TPU v7x, 32 devices: a whole 2x2x4 slice. The times are simulated.
32 devices in a mesh: ep: 4 (over y, x), fsdp: 8 (over z, core).
Axes of the slice: x: 2, y: 2, z: 4, core: 2. Of those that a mesh axis runs over, the one named last changes fastest.
Arguments:
- w_gate: float32 [64, 2048, 1024], P('ep', 'fsdp'), may hold values from -0.1875 to 0.1875
- avg_gate: bfloat16 [64, 2048, 1024], P('ep', 'fsdp'), may hold values from -0.0625 to 0.0625
- w_up: float32 [64, 2048, 1024], P('ep', 'fsdp'), may hold values from -0.1875 to 0.1875
- avg_up: bfloat16 [64, 2048, 1024], P('ep', 'fsdp'), may hold values from -0.0625 to 0.0625
- w_down: float32 [64, 1024, 2048], P('ep', None, 'fsdp'), may hold values from -0.25 to 0.25
- avg_down: bfloat16 [64, 1024, 2048], P('ep', None, 'fsdp'), may hold values from -0.09375 to 0.09375
- router_weight: float32 [2048, 64], P('fsdp', 'ep'), may hold values from -0.125 to 0.125
- router_gain: float32 [2048], P('fsdp'), may hold values from 0.25 to 1.75
Outputs:
- serve_gate: bfloat16 [64, 2048, 1024], P('ep', None, 'fsdp')
- serve_up: bfloat16 [64, 2048, 1024], P('ep', None, 'fsdp')
- serve_down: bfloat16 [64, 1024, 2048], P('ep', 'fsdp')
- scale_gate: float32 [64, 1024], P('ep', 'fsdp')
- scale_up: float32 [64, 1024], P('ep', 'fsdp')
- scale_down: float32 [64, 1024], P('ep', 'fsdp')
- serve_router: bfloat16 [2048, 64], replicated
All inputs are finite; a program needn't handle non-finite values.
Results may differ from a plain program's by a relative error of at most 0.001.
Values may be sent and summed in bfloat16 or wider, within the bound.
A program may use at most 192 MiB of HBM per device.

v0:
```python
import jax
import jax.numpy as jnp
from jax import lax
from jax.sharding import PartitionSpec as P


def on_device(w_gate, avg_gate, w_up, avg_up, w_down, avg_down, router_weight, router_gain):
    fresh_gate = w_gate + avg_gate.astype(jnp.float32)
    fresh_up = w_up + avg_up.astype(jnp.float32)
    fresh_down = w_down + avg_down.astype(jnp.float32)
    total_gate, total_up, total_down = lax.psum(
        (
            jnp.sum(fresh_gate * fresh_gate, axis=1),
            jnp.sum(fresh_up * fresh_up, axis=1),
            jnp.sum(fresh_down * fresh_down, axis=2),
        ),
        "fsdp",
    )
    scale_gate = jnp.sqrt(total_gate)
    scale_up = jnp.sqrt(total_up)
    scale_down = jnp.sqrt(total_down)
    narrow_gate, narrow_up, narrow_down = (
        (fresh_gate / jnp.expand_dims(scale_gate, 1)).astype(jnp.bfloat16),
        (fresh_up / jnp.expand_dims(scale_up, 1)).astype(jnp.bfloat16),
        (fresh_down / jnp.expand_dims(scale_down, 2)).astype(jnp.bfloat16),
    )
    serve_gate, serve_up = (
        lax.all_to_all(narrow_gate, "fsdp", split_axis=2, concat_axis=1, tiled=True),
        lax.all_to_all(narrow_up, "fsdp", split_axis=2, concat_axis=1, tiled=True),
    )
    serve_down = lax.all_to_all(narrow_down, "fsdp", split_axis=1, concat_axis=2, tiled=True)
    scale_gate = lax.dynamic_slice_in_dim(
        scale_gate, lax.axis_index("fsdp") * serve_gate.shape[2], serve_gate.shape[2], axis=1
    )
    scale_up = lax.dynamic_slice_in_dim(
        scale_up, lax.axis_index("fsdp") * serve_up.shape[2], serve_up.shape[2], axis=1
    )
    scale_down = lax.dynamic_slice_in_dim(
        scale_down, lax.axis_index("fsdp") * serve_down.shape[1], serve_down.shape[1], axis=1
    )
    part_router = (router_weight * router_gain[:, None]).astype(jnp.bfloat16)
    row_router = lax.all_gather(part_router, "fsdp", axis=0, tiled=True)
    serve_router = lax.all_gather(row_router, "ep", axis=1, tiled=True)
    return (serve_gate, serve_up, serve_down, scale_gate, scale_up, scale_down, serve_router)


def solution(mesh):
    placed = (
        P("ep", "fsdp", None),
        P("ep", "fsdp", None),
        P("ep", "fsdp", None),
        P("ep", "fsdp", None),
        P("ep", None, "fsdp"),
        P("ep", None, "fsdp"),
        P("fsdp", "ep"),
        P("fsdp"),
    )
    return jax.shard_map(
        on_device,
        mesh=mesh,
        in_specs=placed,
        out_specs=(
            P("ep", None, "fsdp"),
            P("ep", None, "fsdp"),
            P("ep", "fsdp", None),
            P("ep", "fsdp"),
            P("ep", "fsdp"),
            P("ep", "fsdp"),
            P(),
        ),
        check_vma=False,
    )
```

profile of v0, /device:TPU:0, one launch (start us, length us, event | category | flops | bytes accessed | tf_op | source)
XLA Modules:
  0.0 824.8 jit_solution(4685212397091970850)
XLA Ops:
  7.2 0.0 all-reduce.3.cloned.1.call-start
  7.2 17.6 %copy.31 = f32[16,256,1024]{1,0,2:T(8,128)} copy(f32[16,256,1024]{2,1,0:T(8,128)} %param.8) | data formatting | bytes 33554432 | tf_op args[0]
  24.8 17.6 %copy.34 = f32[16,256,1024]{1,0,2:T(8,128)} copy(f32[16,256,1024]{2,1,0:T(8,128)} %param.10) | data formatting | bytes 33554432 | tf_op args[2]
  42.4 12.5 %copy.30 = bf16[16,256,1024]{1,0,2:T(8,128)(2,1)} copy(bf16[16,256,1024]{2,1,0:T(8,128)(2,1)} %param.9) | data formatting | bytes 16777216 | tf_op args[1]
  54.9 12.5 %copy.33 = bf16[16,256,1024]{1,0,2:T(8,128)(2,1)} copy(bf16[16,256,1024]{2,1,0:T(8,128)(2,1)} %param.11) | data formatting | bytes 16777216 | tf_op args[3]
  67.4 0.0 copy-start
  67.4 0.0 copy-start.1
  67.4 25.2 %multiply_reduce_fusion = f32[16,1024]{0,1:T(8,128)} fusion(f32[16,1024,256]{2,1,0:T(8,128)} %param.12, bf16[16,1024,256]{2,1,0:T(8,128)(2,1)} %param.13), kind=kLoop, calls=%fused_computation.2 | loop fusion | flops 16760832 | bytes 25231360 | tf_op jit(solution)/shard_map/reduce_sum | solution.py:15
  92.6 0.0 copy-done
  92.6 0.0 copy-done.1
  92.6 13.2 %multiply_reduce_fusion.1 = (f32[16,1024]{0,1:T(8,128)}, f32[16,1024]{0,1:T(8,128)}) fusion(f32[16,256,1024]{1,0,2:T(8,128)} %copy.34, bf16[16,256,1024]{1,0,2:T(8,128)(2,1)S(1)} %copy-done.1, f32[16,256,1024]{1,0,2:T(8,128)} %copy.31, bf16[16,256,1024]{1,0,2:T(8,128)(2,1)S(1)} %copy-done), kind=kLoop, calls=%fused_computation.4 | loop fusion | flops 33521664 | bytes 50462720 | tf_op jit(solution)/shard_map/reduce_sum | solution.py:14
  105.8 0.0 all-reduce.3.cloned.1.call-update
  105.8 65.1 %all-reduce.3.cloned.1.call-done = (f32[16,1024]{0,1:T(8,128)}, f32[16,1024]{0,1:T(8,128)}, f32[16,1024]{0,1:T(8,128)}) async-done(((f32[16,1024]{0,1:T(8,128)}, f32[16,1024]{0,1:T(8,128)}, f32[16,1024]{0,1:T(8,128)}), (f32[16,1024]{0,1:T(8,128)}, f32[16,1024]{0,1:T(8,128)}, f32[16,1024]{0,1:T(8,128)})) %all-reduce.3.cloned.1.call-update) | async-done | bytes 196624 | tf_op jit(solution)/shard_map/psum | solution.py:11
  170.9 1.2 sqrt.10
  172.1 12.0 %divide_convert_fusion.1 = bf16[16,256,1024]{1,0,2:T(8,128)(2,1)} fusion(f32[16,256,1024]{1,0,2:T(8,128)} %copy.34, bf16[16,256,1024]{1,0,2:T(8,128)(2,1)} %copy.33, f32[16,1024]{0,1:T(8,128)S(1)} %sqrt.10), kind=kLoop, calls=%fused_computation.3 | loop fusion | flops 16777216 | bytes 33619968 | tf_op jit(solution)/shard_map/convert_element_type | solution.py:24
  184.1 0.0 copy-start.3
  184.1 5.1 all-to-all-start.1
  189.2 0.0 copy-done.3
  189.2 0.1 sqrt.9
  189.3 12.0 %divide_convert_fusion.2 = bf16[16,256,1024]{1,0,2:T(8,128)(2,1)} fusion(f32[16,256,1024]{1,0,2:T(8,128)} %copy.31, bf16[16,256,1024]{1,0,2:T(8,128)(2,1)} %copy.30, f32[16,1024]{0,1:T(8,128)S(1)} %sqrt.9), kind=kLoop, calls=%fused_computation.6 | loop fusion | flops 16777216 | bytes 33619968 | tf_op jit(solution)/shard_map/convert_element_type | solution.py:23
  201.3 0.0 copy-start.2
  201.3 171.7 %all-to-all-done.1 = bf16[16,256,1024]{1,0,2:T(8,128)(2,1)} async-done(((bf16[16,256,1024]{1,0,2:T(8,128)(2,1)}), bf16[16,256,1024]{1,0,2:T(8,128)(2,1)}, u32[]{:S(2)}, u32[]{:S(2)}) %all-to-all-start.1) | async-done | bytes 8388640 | tf_op jit(solution)/shard_map/all_to_all | solution.py:29
  373.0 5.1 all-to-all-start
  378.2 0.0 copy-done.2
  378.2 0.1 sqrt.11
  378.3 23.8 %divide_convert_fusion = bf16[16,1024,256]{2,0,1:T(8,128)(2,1)} fusion(f32[16,1024,256]{2,1,0:T(8,128)} %param.12, f32[16,1024]{0,1:T(8,128)S(1)} %sqrt.11, bf16[16,1024,256]{2,1,0:T(8,128)(2,1)} %param.13), kind=kLoop, calls=%fused_computation.1 | loop fusion | flops 16777216 | bytes 33619968 | tf_op jit(solution)/shard_map/convert_element_type | solution.py:25
  402.1 0.0 copy-start.4
  402.1 0.0 copy-start.5
  402.1 159.8 %all-to-all-done = bf16[16,256,1024]{1,0,2:T(8,128)(2,1)} async-done(((bf16[16,256,1024]{1,0,2:T(8,128)(2,1)}), bf16[16,256,1024]{1,0,2:T(8,128)(2,1)}, u32[]{:S(2)}, u32[]{:S(2)}) %all-to-all-start) | async-done | bytes 8388640 | tf_op jit(solution)/shard_map/all_to_all | solution.py:28
  561.8 5.0 all-to-all-start.2
  566.9 0.0 copy-done.4
  566.9 0.0 copy-done.5
  566.9 189.9 %all_gather.6 = bf16[2048,16]{0,1:T(8,128)(2,1)S(1)} all-gather(bf16[256,16]{0,1:T(8,128)(2,1)S(1)} %multiply_convert_fusion), channel_id=1, replica_groups=mesh['ep'=4,'fsdp'=8] {'fsdp'}, dimensions={0}, use_global_device_ids=true | all-gather | bytes 73728 | tf_op jit(solution)/shard_map/all_gather | solution.py:42
  756.8 9.1 %all_gather.7 = bf16[2048,64]{0,1:T(8,128)(2,1)S(1)} all-gather(bf16[2048,16]{0,1:T(8,128)(2,1)S(1)} %all_gather.6), channel_id=1, replica_groups=mesh['ep'=4,'fsdp'=8] {'ep'}, dimensions={1}, use_global_device_ids=true | all-gather | bytes 327680 | tf_op jit(solution)/shard_map/all_gather | solution.py:43
  765.9 0.7 copy.39
  766.6 0.7 copy.40
  767.3 0.7 copy.41
  767.9 12.3 %copy.35 = bf16[16,8,256,128]{3,2,1,0:T(8,128)(2,1)} copy(bf16[16,8,256,128]{2,0,3,1:T(8,128)(2,1)} %bitcast.4) | data formatting | bytes 16777216 | tf_op jit(solution)/shard_map/all_to_all | solution.py:29
  780.2 12.3 %copy.32 = bf16[16,8,256,128]{3,2,1,0:T(8,128)(2,1)} copy(bf16[16,8,256,128]{2,0,3,1:T(8,128)(2,1)} %bitcast.1) | data formatting | bytes 16777216 | tf_op jit(solution)/shard_map/all_to_all | solution.py:28
  792.5 0.0 all-to-all-done.2
  792.5 11.4 %copy.38 = bf16[16,128,8,256]{3,2,1,0:T(8,128)(2,1)} copy(bf16[16,128,8,256]{3,0,1,2:T(8,128)(2,1)} %bitcast.7) | data formatting | bytes 16777216 | tf_op jit(solution)/shard_map/all_to_all | solution.py:31
  803.9 13.4 %all_to_all.50 = bf16[16,128,2048]{2,1,0:T(8,128)(2,1)} reshape(bf16[16,128,8,256]{3,2,1,0:T(8,128)(2,1)} %copy.38) | data formatting | bytes 16777216 | tf_op jit(solution)/shard_map/all_to_all | solution.py:31
  817.3 0.7 copy.53
  (4 shorter events, 0.0 us)
Async XLA Ops:
  7.2 163.7 %all-reduce.3.cloned.1.call-start = ((), (), s32[]{:S(2)}) async-start(), calls=%async_computation.3 | async-start | bytes 3145728 | tf_op jit(solution)/shard_map/psum | solution.py:11
  67.4 25.2 %copy-start = (bf16[16,256,1024]{1,0,2:T(8,128)(2,1)S(1)}, bf16[16,256,1024]{1,0,2:T(8,128)(2,1)}, u32[]{:S(2)}) copy-start(bf16[16,256,1024]{1,0,2:T(8,128)(2,1)} %copy.30) | copy-start | bytes 25165828
  67.4 25.2 %copy-start.1 = (bf16[16,256,1024]{1,0,2:T(8,128)(2,1)S(1)}, bf16[16,256,1024]{1,0,2:T(8,128)(2,1)}, u32[]{:S(2)}) copy-start(bf16[16,256,1024]{1,0,2:T(8,128)(2,1)} %copy.33) | copy-start | bytes 25165828
  184.1 5.1 copy-start.3
  184.1 189.0 %all-to-all-start.1 = ((bf16[16,256,1024]{1,0,2:T(8,128)(2,1)}), bf16[16,256,1024]{1,0,2:T(8,128)(2,1)}, u32[]{:S(2)}, u32[]{:S(2)}) async-start(bf16[16,256,1024]{1,0,2:T(8,128)(2,1)} %divide_convert_fusion.1), calls=%async_computation.1 | async-start | bytes 16777216 | tf_op jit(solution)/shard_map/all_to_all | solution.py:29
  201.3 176.9 %copy-start.2 = (f32[16,1024]{0,1:T(8,128)S(1)}, f32[16,1024]{0,1:T(8,128)}, u32[]{:S(2)}) copy-start(f32[16,1024]{0,1:T(8,128)} %get-tuple-element.16) | copy-start | bytes 196612
  373.0 188.8 %all-to-all-start = ((bf16[16,256,1024]{1,0,2:T(8,128)(2,1)}), bf16[16,256,1024]{1,0,2:T(8,128)(2,1)}, u32[]{:S(2)}, u32[]{:S(2)}) async-start(bf16[16,256,1024]{1,0,2:T(8,128)(2,1)} %divide_convert_fusion.2), calls=%async_computation | async-start | bytes 16777216 | tf_op jit(solution)/shard_map/all_to_all | solution.py:28
  402.1 164.8 %copy-start.4 = (f32[256,16]{0,1:T(8,128)S(1)}, f32[256,16]{0,1:T(8,128)}, u32[]{:S(2)}) copy-start(f32[256,16]{0,1:T(8,128)} %param.14) | copy-start | bytes 49156
  402.1 164.8 %copy-start.5 = (f32[256]{0:T(256)S(1)}, f32[256]{0:T(256)}, u32[]{:S(2)}) copy-start(f32[256]{0:T(256)} %param.15) | copy-start | bytes 3076
  561.8 230.7 %all-to-all-start.2 = ((bf16[16,1024,256]{2,0,1:T(8,128)(2,1)}), bf16[16,1024,256]{2,0,1:T(8,128)(2,1)}, u32[]{:S(2)}, u32[]{:S(2)}) async-start(bf16[16,1024,256]{2,0,1:T(8,128)(2,1)} %divide_convert_fusion), calls=%async_computation.2 | async-start | bytes 16777216 | tf_op jit(solution)/shard_map/all_to_all | solution.py:31
Sparse Core Ops, SparseCore 0:
  105.9 64.9 all-reduce.2
where the time goes:
time: 827 us; the launch traced here: 825 us
  waiting for transfers between devices  397 us (48%)
  blocking collectives  199 us (24%)
  local copies, waits for them, and re-layouts  114 us (14%)
  other arithmetic  86.1 us (10%)
  starting transfers between devices  15.3 us (2%)
  between operations  14.1 us (2%)
    all_gather x1, blocking collectives, on_device(): row_router = lax.all_gather(part_router, 'fsdp', axis=0, tiled=True)  190 us
    all_to_all x1, waiting for transfers between devices, on_device(): lax.all_to_all(narrow_up, 'fsdp', split_axis=2, concat_axis=1, tiled=True)  172 us
    all_to_all x1, waiting for transfers between devices, on_device(): lax.all_to_all(narrow_gate, 'fsdp', split_axis=2, concat_axis=1, tiled=True)  160 us
    psum x1, waiting for transfers between devices, on_device(): lax.psum((jnp.sum(fresh_gate * fresh_gate, axis=1), jnp.sum(fresh_up * fr...  65.1 us
    unnamed x20, local copies, waits for them, and re-layouts  62.9 us
    reduce_sum x1, other arithmetic, on_device(): jnp.sum(fresh_down * fresh_down, axis=2)  25.2 us
    all_to_all x2, local copies, waits for them, and re-layouts, on_device(): lax.all_to_all(narrow_down, 'fsdp', split_axis=1, concat_axis=2, tiled=True)  24.8 us
    convert_element_type x1, other arithmetic, on_device(): (fresh_down / jnp.expand_dims(scale_down, 2)).astype(jnp.bfloat16)  23.8 us
  transfers between devices with their start and end apart: 4, of which 3 were waited for; matrix products, arithmetic and copies ran while one was open for 8% of the time, Pallas kernels for 0%

commit v1 on v0

--- a/solution.py
+++ b/solution.py
@@ -24,9 +24,15 @@
         (fresh_up / jnp.expand_dims(scale_up, 1)).astype(jnp.bfloat16),
         (fresh_down / jnp.expand_dims(scale_down, 2)).astype(jnp.bfloat16),
     )
+    refer_side = lambda panel, dev_axis: jnp.concatenate(
+        jax.lax.all_to_all(
+            jnp.stack(jnp.split(panel, jax.lax.psum(1, dev_axis), 2), axis=0), dev_axis, 0, 0
+        ),
+        1,
+    )
     serve_gate, serve_up = (
         lax.all_to_all(narrow_gate, "fsdp", split_axis=2, concat_axis=1, tiled=True),
-        lax.all_to_all(narrow_up, "fsdp", split_axis=2, concat_axis=1, tiled=True),
+        refer_side(narrow_up, "fsdp"),
     )
     serve_down = lax.all_to_all(narrow_down, "fsdp", split_axis=1, concat_axis=2, tiled=True)
     scale_gate = lax.dynamic_slice_in_dim(

time: 827 us -> 789 us (0.954)
  local copies, waits for them, and re-layouts: 114 us -> 89 us
  waiting for transfers between devices: 397 us -> 387 us
    unnamed x20 -> x28, local copies, waits for them, and re-layouts: 62.9 us -> 40.9 us
    all_to_all x1 -> x0, local copies, waits for them, and re-layouts: 12.3 us -> none  [on_device(): lax.all_to_all(narrow_up, 'fsdp', split_axis=2, concat_axis=1, tiled=True)]
    all_to_all x1, waiting for transfers between devices: 172 us -> 160 us  [on_device(): jax.lax.all_to_all(jnp.stack(jnp.split(panel, jax.lax.psum(1, dev_axis),...]
    reduce_sum x0 -> x1, other arithmetic: none -> 10.6 us  [on_device(): jnp.sum(fresh_gate * fresh_gate, axis=1)]
    reduce_sum x1, other arithmetic: 25.2 us -> 16.8 us  [on_device(): jnp.sum(fresh_down * fresh_down, axis=2)]
where the time goes in v1:
time: 789 us; the launch traced here: 788 us
  waiting for transfers between devices  387 us (49%)
  blocking collectives  199 us (25%)
  local copies, waits for them, and re-layouts  89 us (11%)
  other arithmetic  83.6 us (11%)
  starting transfers between devices  15.3 us (2%)
  between operations  14.2 us (2%)
    all_gather x1, blocking collectives, on_device(): row_router = lax.all_gather(part_router, 'fsdp', axis=0, tiled=True)  190 us
    all_to_all x1, waiting for transfers between devices, on_device(): lax.all_to_all(narrow_gate, 'fsdp', split_axis=2, concat_axis=1, tiled=True)  164 us
    all_to_all x1, waiting for transfers between devices, on_device(): jax.lax.all_to_all(jnp.stack(jnp.split(panel, jax.lax.psum(1, dev_axis),...  160 us
    psum x1, waiting for transfers between devices, on_device(): lax.psum((jnp.sum(fresh_gate * fresh_gate, axis=1), jnp.sum(fresh_up * fr...  62.6 us
    unnamed x28, local copies, waits for them, and re-layouts  40.9 us
    all_to_all x2, local copies, waits for them, and re-layouts, on_device(): lax.all_to_all(narrow_down, 'fsdp', split_axis=1, concat_axis=2, tiled=True)  24.8 us
    convert_element_type x1, other arithmetic, on_device(): (fresh_down / jnp.expand_dims(scale_down, 2)).astype(jnp.bfloat16)  23.8 us
    reduce_sum x1, other arithmetic, on_device(): jnp.sum(fresh_down * fresh_down, axis=2)  16.8 us
  transfers between devices with their start and end apart: 4, of which 3 were waited for; matrix products, arithmetic and copies ran while one was open for 8% of the time, Pallas kernels for 0%

profile of v1, /device:TPU:0, one launch (start us, length us, event | category | flops | bytes accessed | tf_op | source)
XLA Modules:
  0.0 787.9 jit_solution(3974083231037796088)
XLA Ops:
  7.2 0.0 all-reduce.3.cloned.1.call-start
  7.2 17.6 %copy.28 = f32[16,256,1024]{1,0,2:T(8,128)} copy(f32[16,256,1024]{2,1,0:T(8,128)} %param.8) | data formatting | bytes 33554432 | tf_op args[0]
  24.8 12.5 %copy.27 = bf16[16,256,1024]{1,0,2:T(8,128)(2,1)} copy(bf16[16,256,1024]{2,1,0:T(8,128)(2,1)} %param.9) | data formatting | bytes 16777216 | tf_op args[1]
  37.3 0.0 slice-start
  37.3 0.0 slice-start.1
  37.3 0.0 slice-start.2
  37.3 10.6 %multiply_reduce_fusion.2 = f32[16,1024]{0,1:T(8,128)} fusion(f32[16,256,1024]{1,0,2:T(8,128)} %copy.28, bf16[16,256,1024]{1,0,2:T(8,128)(2,1)} %copy.27), kind=kLoop, calls=%fused_computation.7 | loop fusion | flops 16760832 | bytes 25231360 | tf_op jit(solution)/shard_map/reduce_sum | solution.py:13
  48.0 0.0 slice-start.3
  48.0 11.0 %multiply_reduce_fusion.1 = f32[16,1024]{1,0:T(8,128)} fusion(f32[16,256,1024]{2,1,0:T(8,128)} %param.10, bf16[16,256,1024]{2,1,0:T(8,128)(2,1)} %param.11), kind=kLoop, calls=%fused_computation.4 | loop fusion | flops 16760832 | bytes 25231360 | tf_op jit(solution)/shard_map/reduce_sum | solution.py:14
  59.0 0.0 slice-done
  59.0 0.0 slice-done.1
  59.0 0.0 slice-done.2
  59.0 0.0 slice-done.3
  59.0 16.8 %multiply_reduce_fusion = f32[16,1024]{0,1:T(8,128)} fusion(f32[16,1024,256]{2,1,0:T(8,128)S(1)} %bitcast.44, bf16[16,1024,256]{2,1,0:T(8,128)(2,1)} %param.13), kind=kLoop, calls=%fused_computation.2 | loop fusion | flops 16760832 | bytes 25231360 | tf_op jit(solution)/shard_map/reduce_sum | solution.py:15
  75.7 0.0 all-reduce.3.cloned.1.call-update
  75.8 62.6 %all-reduce.3.cloned.1.call-done = (f32[16,1024]{0,1:T(8,128)}, f32[16,1024]{1,0:T(8,128)}, f32[16,1024]{0,1:T(8,128)}) async-done(((f32[16,1024]{0,1:T(8,128)}, f32[16,1024]{1,0:T(8,128)}, f32[16,1024]{0,1:T(8,128)}), (f32[16,1024]{0,1:T(8,128)}, f32[16,1024]{1,0:T(8,128)}, f32[16,1024]{0,1:T(8,128)})) %all-reduce.3.cloned.1.call-update) | async-done | bytes 196624 | tf_op jit(solution)/shard_map/psum | solution.py:11
  138.4 1.2 sqrt.9
  139.6 12.0 %divide_convert_fusion.2 = bf16[16,256,1024]{1,0,2:T(8,128)(2,1)} fusion(f32[16,256,1024]{1,0,2:T(8,128)} %copy.28, bf16[16,256,1024]{1,0,2:T(8,128)(2,1)} %copy.27, f32[16,1024]{0,1:T(8,128)S(1)} %sqrt.9), kind=kLoop, calls=%fused_computation.6 | loop fusion | flops 16777216 | bytes 33619968 | tf_op jit(solution)/shard_map/convert_element_type | solution.py:23
  151.5 0.0 copy-start.1
  151.5 5.1 all-to-all-start
  156.6 0.0 copy-done.1
  156.7 9.4 %divide_convert_fusion.1 = bf16[16,256,1024]{2,1,0:T(8,128)(2,1)S(1)} fusion(f32[16,256,1024]{2,1,0:T(8,128)} %param.10, bf16[16,256,1024]{2,1,0:T(8,128)(2,1)} %param.11, f32[16,1024]{1,0:T(8,128)S(1)} %sqrt.10), kind=kLoop, calls=%fused_computation.3 | loop fusion | flops 16777216 | bytes 33619968 | tf_op jit(solution)/shard_map/convert_element_type | solution.py:24
  166.1 1.2 fusion.7
  167.3 1.2 fusion.6
  168.6 1.2 fusion.5
  169.8 1.2 fusion.4
  171.1 1.2 fusion.3
  172.3 1.2 fusion.2
  173.6 1.2 fusion.1
  174.8 1.2 fusion
  176.1 0.0 copy-start
  176.1 164.4 %all-to-all-done = bf16[16,256,1024]{1,0,2:T(8,128)(2,1)} async-done(((bf16[16,256,1024]{1,0,2:T(8,128)(2,1)}), bf16[16,256,1024]{1,0,2:T(8,128)(2,1)}, u32[]{:S(2)}, u32[]{:S(2)}) %all-to-all-start) | async-done | bytes 8388640 | tf_op jit(solution)/shard_map/all_to_all | solution.py:34
  340.5 5.2 all-to-all-start.1
  345.7 0.0 copy-done
  345.7 0.1 sqrt.11
  345.9 23.8 %divide_convert_fusion = bf16[16,1024,256]{2,0,1:T(8,128)(2,1)} fusion(f32[16,1024,256]{2,1,0:T(8,128)} %param.12, f32[16,1024]{0,1:T(8,128)S(1)} %sqrt.11, bf16[16,1024,256]{2,1,0:T(8,128)(2,1)} %param.13), kind=kLoop, calls=%fused_computation.1 | loop fusion | flops 16777216 | bytes 33619968 | tf_op jit(solution)/shard_map/convert_element_type | solution.py:25
  369.6 0.0 copy-start.2
  369.6 0.0 copy-start.3
  369.7 159.7 %all-to-all-done.1 = bf16[8,16,256,128]{3,2,1,0:T(8,128)(2,1)} async-done(((bf16[8,16,256,128]{3,2,1,0:T(8,128)(2,1)}), bf16[8,16,256,128]{3,2,1,0:T(8,128)(2,1)}, u32[]{:S(2)}, u32[]{:S(2)}) %all-to-all-start.1) | async-done | bytes 8388640 | tf_op jit(solution)/shard_map/all_to_all | solution.py:28
  529.4 5.0 all-to-all-start.2
  534.4 0.0 copy-done.2
  534.4 0.0 copy-done.3
  534.4 189.9 %all_gather.6 = bf16[2048,16]{0,1:T(8,128)(2,1)S(1)} all-gather(bf16[256,16]{0,1:T(8,128)(2,1)S(1)} %multiply_convert_fusion), channel_id=1, replica_groups=mesh['ep'=4,'fsdp'=8] {'fsdp'}, dimensions={0}, use_global_device_ids=true | all-gather | bytes 73728 | tf_op jit(solution)/shard_map/all_gather | solution.py:48
  724.3 9.1 %all_gather.7 = bf16[2048,64]{0,1:T(8,128)(2,1)S(1)} all-gather(bf16[2048,16]{0,1:T(8,128)(2,1)S(1)} %all_gather.6), channel_id=1, replica_groups=mesh['ep'=4,'fsdp'=8] {'ep'}, dimensions={1}, use_global_device_ids=true | all-gather | bytes 327680 | tf_op jit(solution)/shard_map/all_gather | solution.py:49
  733.4 0.7 copy.34
  734.1 0.7 copy.35
  734.8 0.6 constant_dynamic-slice_fusion.1
  735.4 12.3 %copy.29 = bf16[16,8,256,128]{3,2,1,0:T(8,128)(2,1)} copy(bf16[16,8,256,128]{2,0,3,1:T(8,128)(2,1)} %bitcast.1) | data formatting | bytes 16777216 | tf_op jit(solution)/shard_map/all_to_all | solution.py:34
  747.6 7.9 %copy.30 = bf16[16,8,256,128]{3,2,1,0:T(8,128)(2,1)} copy(bf16[16,8,256,128]{3,2,0,1:T(8,128)(2,1)} %bitcast.11) | data formatting | bytes 16777216 | tf_op jit(solution)/shard_map/reshape | solution.py:27
  755.5 0.0 all-to-all-done.2
  755.5 11.4 %copy.33 = bf16[16,128,8,256]{3,2,1,0:T(8,128)(2,1)} copy(bf16[16,128,8,256]{3,0,1,2:T(8,128)(2,1)} %bitcast.14) | data formatting | bytes 16777216 | tf_op jit(solution)/shard_map/all_to_all | solution.py:37
  766.9 13.4 %all_to_all.37 = bf16[16,128,2048]{2,1,0:T(8,128)(2,1)} reshape(bf16[16,128,8,256]{3,2,1,0:T(8,128)(2,1)} %copy.33) | data formatting | bytes 16777216 | tf_op jit(solution)/shard_map/all_to_all | solution.py:37
  780.3 0.7 copy.54
  (4 shorter events, 0.0 us)
Async XLA Ops:
  7.2 131.2 %all-reduce.3.cloned.1.call-start = ((), (), s32[]{:S(2)}) async-start(), calls=%async_computation.3 | async-start | bytes 2228224 | tf_op jit(solution)/shard_map/psum | solution.py:11
  37.3 21.7 %slice-start = ((s8[16777216]{0:T(1024)(128)(4,1)}), s8[4194304]{0:T(1024)(128)(4,1)S(1)}, s32[]{:S(2)}) async-start(s8[16777216]{0:T(1024)(128)(4,1)} %bitcast.43), calls=%async_computation.4 | async-start | bytes 8388608
  37.3 21.7 %slice-start.1 = ((s8[16777216]{0:T(1024)(128)(4,1)}), s8[4194304]{0:T(1024)(128)(4,1)S(1)}, s32[]{:S(2)}) async-start(s8[16777216]{0:T(1024)(128)(4,1)} %bitcast.43), calls=%async_computation.5 | async-start | bytes 8388608
  37.3 21.7 %slice-start.2 = ((s8[16777216]{0:T(1024)(128)(4,1)}), s8[4194304]{0:T(1024)(128)(4,1)S(1)}, s32[]{:S(2)}) async-start(s8[16777216]{0:T(1024)(128)(4,1)} %bitcast.43), calls=%async_computation.6 | async-start | bytes 8388608
  48.0 11.0 %slice-start.3 = ((s8[16777216]{0:T(1024)(128)(4,1)}), s8[4194304]{0:T(1024)(128)(4,1)S(1)}, s32[]{:S(2)}) async-start(s8[16777216]{0:T(1024)(128)(4,1)} %bitcast.43), calls=%async_computation.7 | async-start | bytes 8388608
  151.5 5.1 copy-start.1
  151.5 188.9 %all-to-all-start = ((bf16[16,256,1024]{1,0,2:T(8,128)(2,1)}), bf16[16,256,1024]{1,0,2:T(8,128)(2,1)}, u32[]{:S(2)}, u32[]{:S(2)}) async-start(bf16[16,256,1024]{1,0,2:T(8,128)(2,1)} %divide_convert_fusion.2), calls=%async_computation | async-start | bytes 16777216 | tf_op jit(solution)/shard_map/all_to_all | solution.py:34
  176.1 169.7 %copy-start = (f32[16,1024]{0,1:T(8,128)S(1)}, f32[16,1024]{0,1:T(8,128)}, u32[]{:S(2)}) copy-start(f32[16,1024]{0,1:T(8,128)} %get-tuple-element.16) | copy-start | bytes 196612
  340.5 188.9 %all-to-all-start.1 = ((bf16[8,16,256,128]{3,2,1,0:T(8,128)(2,1)}), bf16[8,16,256,128]{3,2,1,0:T(8,128)(2,1)}, u32[]{:S(2)}, u32[]{:S(2)}) async-start(bf16[8,16,256,128]{3,2,1,0:T(8,128)(2,1)} %fusion), calls=%async_computation.1 | async-start | bytes 16777216 | tf_op jit(solution)/shard_map/all_to_all | solution.py:28
  369.6 164.7 %copy-start.2 = (f32[256,16]{0,1:T(8,128)S(1)}, f32[256,16]{0,1:T(8,128)}, u32[]{:S(2)}) copy-start(f32[256,16]{0,1:T(8,128)} %param.14) | copy-start | bytes 49156
  369.6 164.7 %copy-start.3 = (f32[256]{0:T(256)S(1)}, f32[256]{0:T(256)}, u32[]{:S(2)}) copy-start(f32[256]{0:T(256)} %param.15) | copy-start | bytes 3076
  529.4 226.1 %all-to-all-start.2 = ((bf16[16,1024,256]{2,0,1:T(8,128)(2,1)}), bf16[16,1024,256]{2,0,1:T(8,128)(2,1)}, u32[]{:S(2)}, u32[]{:S(2)}) async-start(bf16[16,1024,256]{2,0,1:T(8,128)(2,1)} %divide_convert_fusion), calls=%async_computation.2 | async-start | bytes 16777216 | tf_op jit(solution)/shard_map/all_to_all | solution.py:37
Sparse Core Ops, SparseCore 0:
  75.9 62.4 all-reduce.2
